TPU v7x, 32 devices: a whole 2x2x4 slice. The times are simulated.
32 devices in a mesh: seq: 16 (over z, y, x), head: 2 (over core).
Axes of the slice: x: 2, y: 2, z: 4, core: 2. Of those that a mesh axis runs over, the one named last changes fastest.
Arguments:
- queries: bfloat16 [32768, 1024], P('seq', 'head'), may hold values from -10 to 10
- key_vectors: bfloat16 [32768, 1024], P('seq', 'head'), may hold values from -10 to 10
- value_vectors: bfloat16 [32768, 1024], P('seq', 'head'), may hold values from -6 to 6
- grad_output: bfloat16 [32768, 1024], P('seq', 'head'), may hold values from -6 to 6
Outputs:
- attended: bfloat16 [32768, 1024], P('seq', 'head')
- grad_queries: bfloat16 [32768, 1024], P('seq', 'head')
- grad_keys: bfloat16 [32768, 1024], P('seq', 'head')
- grad_values: bfloat16 [32768, 1024], P('seq', 'head')
All inputs are finite; a program needn't handle non-finite values.
Results may differ from a plain program's by a relative error of at most 0.019.
Values may be sent and summed in bfloat16 or wider, within the bound.
A program may use at most 128 MiB of HBM per device.

v0:
```python
import math

import jax
import jax.numpy as jnp
from jax import lax
from jax.sharding import PartitionSpec as P

ROW_LEN = 512
HEAD_DIM = 128


NEG_FILL = -1e30


def shortened(x):

    def short(part):
        return part.astype(jnp.bfloat16) if part.dtype == jnp.float32 else part

    return jax.tree.map(short, x)


def head_window(array, index):
    return array[:, index * HEAD_DIM : (index + 1) * HEAD_DIM]


def inner_last(left, right):
    return lax.dot_general(
        left, right, (((1,), (1,)), ((), ())), preferred_element_type=jnp.float32
    )


def inner_first(left, right):
    return lax.dot_general(
        left, right, (((0,), (0,)), ((), ())), preferred_element_type=jnp.float32
    )


def attend_forward(query_block, key_block, value_block, allowed):
    scaling = 1.0 / math.sqrt(HEAD_DIM)
    heads_here = query_block.shape[1] // HEAD_DIM
    sums, maxes, totals = ([], [], [])
    for index in range(heads_here):
        scores = (
            inner_last(head_window(query_block, index), head_window(key_block, index)) * scaling
        )
        maxima = jnp.max(jnp.where(allowed, scores, NEG_FILL), axis=-1)
        weights = jnp.where(allowed, jnp.exp(scores - maxima[:, None]), 0.0)
        totals.append(jnp.sum(weights, axis=-1))
        maxes.append(maxima)
        sums.append(
            jnp.dot(
                weights.astype(jnp.bfloat16),
                head_window(value_block, index),
                preferred_element_type=jnp.float32,
            )
        )
    return (jnp.concatenate(sums, axis=1), jnp.stack(maxes, axis=1), jnp.stack(totals, axis=1))


def attend_backward(
    query_block, key_block, value_block, grad_block, log_totals, correction, allowed
):
    scaling = 1.0 / math.sqrt(HEAD_DIM)
    heads_here = query_block.shape[1] // HEAD_DIM
    parts_query, parts_key, parts_value = ([], [], [])
    for index in range(heads_here):
        query_head = head_window(query_block, index)
        key_head = head_window(key_block, index)
        grad_head = head_window(grad_block, index)
        scores = inner_last(query_head, key_head) * scaling
        probabilities = jnp.where(allowed, jnp.exp(scores - log_totals[:, index][:, None]), 0.0)
        parts_value.append(inner_first(probabilities.astype(jnp.bfloat16), grad_head))
        grad_probs = inner_last(grad_head, head_window(value_block, index))
        grad_scores = (probabilities * (grad_probs - correction[:, index][:, None])).astype(
            jnp.bfloat16
        )
        parts_query.append(
            jnp.dot(grad_scores, key_head, preferred_element_type=jnp.float32) * scaling
        )
        parts_key.append(inner_first(grad_scores, query_head) * scaling)
    return (
        jnp.concatenate(parts_query, axis=1),
        jnp.concatenate(parts_key, axis=1),
        jnp.concatenate(parts_value, axis=1),
    )


def to_sending(array, devices):
    rows_here, length, width = array.shape
    return jnp.transpose(array.reshape(rows_here, devices, length // devices, width), (1, 2, 0, 3))


def from_receiving(array):
    return array.reshape(array.shape[1], array.shape[2], array.shape[3])


def to_returning(array):
    return array.reshape((1,) + array.shape)


def from_returned(array):
    devices, per_dev, rows_here, width = array.shape
    return jnp.transpose(array, (2, 0, 1, 3)).reshape(rows_here, devices * per_dev, width)


def on_device(queries, key_vectors, value_vectors, grad_output):
    devices = lax.axis_size("seq")
    rows_here = queries.shape[0] // ROW_LEN
    width = queries.shape[1]
    heads_here = width // HEAD_DIM
    total_rows = rows_here * devices
    layout = (rows_here, ROW_LEN, width)
    query_rows = queries.reshape(layout)
    key_rows = key_vectors.reshape(layout)
    value_rows = value_vectors.reshape(layout)
    grad_rows = grad_output.reshape(layout)
    column_pos = jnp.arange(ROW_LEN)
    row_allowed = column_pos[None, :] <= column_pos[:, None]
    row_pos = jnp.arange(total_rows)
    column_allowed = row_pos[None, :] < row_pos[:, None]
    sent = (
        lax.all_to_all(
            to_sending(query_rows, devices), "seq", split_axis=0, concat_axis=2, tiled=True
        ),
        lax.all_to_all(
            to_sending(key_rows, devices), "seq", split_axis=0, concat_axis=2, tiled=True
        ),
        lax.all_to_all(
            to_sending(value_rows, devices), "seq", split_axis=0, concat_axis=2, tiled=True
        ),
    )
    query_cols, key_cols, value_cols = (
        from_receiving(sent[0]),
        from_receiving(sent[1]),
        from_receiving(sent[2]),
    )
    row_acc, row_max, row_tot = lax.map(
        lambda blocks: attend_forward(blocks[0], blocks[1], blocks[2], row_allowed),
        (query_rows, key_rows, value_rows),
    )
    col_acc, col_max, col_tot = lax.map(
        lambda blocks: attend_forward(blocks[0], blocks[1], blocks[2], column_allowed),
        (query_cols, key_cols, value_cols),
    )
    col_floor = jnp.maximum(col_tot, 1.0)
    col_out = (
        (col_acc.reshape(col_acc.shape[:2] + (heads_here, HEAD_DIM)) / col_floor[..., None])
        .astype(jnp.bfloat16)
        .reshape(col_acc.shape)
    )
    col_lse = col_max + jnp.log(col_floor)
    back_out = from_returned(
        lax.all_to_all(to_returning(col_out), "seq", split_axis=2, concat_axis=0, tiled=True)
    ).astype(jnp.float32)
    back_lse = from_returned(
        lax.all_to_all(to_returning(col_lse), "seq", split_axis=2, concat_axis=0, tiled=True)
    )
    maxima = jnp.maximum(row_max, back_lse)
    row_weight = jnp.exp(row_max - maxima)
    col_weight = jnp.exp(back_lse - maxima)
    denominators = row_tot * row_weight + col_weight
    split_shape = (rows_here, ROW_LEN, heads_here, HEAD_DIM)
    attended = (
        row_acc.reshape(split_shape) * row_weight[..., None]
        + back_out.reshape(split_shape) * col_weight[..., None]
    ) / denominators[..., None]
    log_totals = maxima + jnp.log(denominators)
    attended_low = attended.astype(jnp.bfloat16)
    correction = jnp.sum(
        grad_rows.reshape(split_shape).astype(jnp.float32) * attended_low.astype(jnp.float32),
        axis=-1,
    )
    again = (
        lax.all_to_all(
            to_sending(query_rows, devices), "seq", split_axis=0, concat_axis=2, tiled=True
        ),
        lax.all_to_all(
            to_sending(key_rows, devices), "seq", split_axis=0, concat_axis=2, tiled=True
        ),
        lax.all_to_all(
            to_sending(value_rows, devices), "seq", split_axis=0, concat_axis=2, tiled=True
        ),
        lax.all_to_all(
            to_sending(grad_rows, devices), "seq", split_axis=0, concat_axis=2, tiled=True
        ),
    )
    query_back, key_back, value_back, grad_cols = (
        from_receiving(again[0]),
        from_receiving(again[1]),
        from_receiving(again[2]),
        from_receiving(again[3]),
    )
    log_sent, corr_sent = (
        lax.all_to_all(
            to_sending(log_totals, devices), "seq", split_axis=0, concat_axis=2, tiled=True
        ),
        lax.all_to_all(
            to_sending(correction, devices), "seq", split_axis=0, concat_axis=2, tiled=True
        ),
    )
    log_cols, corr_cols = (from_receiving(log_sent), from_receiving(corr_sent))
    row_grads = lax.map(
        lambda blocks: attend_backward(
            blocks[0], blocks[1], blocks[2], blocks[3], blocks[4], blocks[5], row_allowed
        ),
        (query_rows, key_rows, value_rows, grad_rows, log_totals, correction),
    )
    col_grads = lax.map(
        lambda blocks: attend_backward(
            blocks[0], blocks[1], blocks[2], blocks[3], blocks[4], blocks[5], column_allowed
        ),
        (query_back, key_back, value_back, grad_cols, log_cols, corr_cols),
    )
    col_low = (
        to_returning(col_grads[0].astype(jnp.bfloat16)),
        to_returning(col_grads[1].astype(jnp.bfloat16)),
        to_returning(col_grads[2].astype(jnp.bfloat16)),
    )
    back_query, back_key, back_value = (
        lax.all_to_all(shortened(col_low[0]), "seq", split_axis=2, concat_axis=0, tiled=True),
        lax.all_to_all(shortened(col_low[1]), "seq", split_axis=2, concat_axis=0, tiled=True),
        lax.all_to_all(shortened(col_low[2]), "seq", split_axis=2, concat_axis=0, tiled=True),
    )
    grad_q = (
        (row_grads[0] + from_returned(back_query).astype(jnp.float32))
        .astype(jnp.bfloat16)
        .reshape(queries.shape)
    )
    grad_k = (
        (row_grads[1] + from_returned(back_key).astype(jnp.float32))
        .astype(jnp.bfloat16)
        .reshape(queries.shape)
    )
    grad_v = (
        (row_grads[2] + from_returned(back_value).astype(jnp.float32))
        .astype(jnp.bfloat16)
        .reshape(queries.shape)
    )
    return (attended_low.reshape(queries.shape), grad_q, grad_k, grad_v)


def solution(mesh):
    placed = (P("seq", "head"), P("seq", "head"), P("seq", "head"), P("seq", "head"))
    return jax.shard_map(
        on_device,
        mesh=mesh,
        in_specs=placed,
        out_specs=(P("seq", "head"), P("seq", "head"), P("seq", "head"), P("seq", "head")),
        check_vma=False,
    )
```

profile of v0, /device:TPU:12, one launch (start us, length us, event | category | flops | bytes accessed | tf_op | source)
XLA Modules:
  0.0 1222.8 jit_solution(7327744043618147651)
XLA Ops:
  0.6 4.7 copy.155
  5.3 7.2 all-to-all-start
  12.5 4.7 copy.157
  17.2 43.5 %all-to-all-done = bf16[16,32,4,512]{3,2,1,0:T(4,128)(2,1)S(1)} async-done(((bf16[16,32,4,512]{3,2,1,0:T(4,128)(2,1)}), bf16[16,32,4,512]{3,2,1,0:T(4,128)(2,1)S(1)}, u32[]{:S(2)}, u32[]{:S(2)}) %all-to-all-start) | async-done | bytes 2097184 | tf_op jit(solution)/shard_map/all_to_all | solution.py:123
  60.6 4.9 all-to-all-start.1
  65.5 4.7 copy.159
  70.2 43.0 %all-to-all-done.1 = bf16[16,32,4,512]{3,2,1,0:T(4,128)(2,1)} async-done(((bf16[16,32,4,512]{3,2,1,0:T(4,128)(2,1)}), bf16[16,32,4,512]{3,2,1,0:T(4,128)(2,1)}, u32[]{:S(2)}, u32[]{:S(2)}) %all-to-all-start.1) | async-done | bytes 2097184 | tf_op jit(solution)/shard_map/all_to_all | solution.py:126
  113.2 5.4 all-to-all-start.2
  125.1 41.1 %all-to-all-done.2 = bf16[16,32,4,512]{3,2,1,0:T(4,128)(2,1)} async-done(((bf16[16,32,4,512]{3,2,1,0:T(4,128)(2,1)}), bf16[16,32,4,512]{3,2,1,0:T(4,128)(2,1)}, u32[]{:S(2)}, u32[]{:S(2)}) %all-to-all-start.2) | async-done | bytes 2097184 | tf_op jit(solution)/shard_map/all_to_all | solution.py:129
  170.8 208.6 %while.69 = (s32[]{:T(128)}, f32[32,64,512]{2,0,1:T(8,128)}, f32[32,64,4]{1,0,2:T(8,128)S(1)}, f32[32,64,4]{1,0,2:T(8,128)S(1)}, bf16[32,64,512]{2,1,0:T(8,128)(...) while((s32[]{:T(128)}, f32[32,64,512]{2,0,1:T(8,128)}, ...), condition=%wide.region_19.20_spmd.clone.clone.clone, body=%wide.region_10.19_spmd.clone.clone.sunk.clone | while | flops 8684546 | bytes 1782889 | solution.py:142
  277.3 3.8 dynamic_update_slice.97
  283.9 3.8 dynamic_update_slice.97
  290.4 3.8 dynamic_update_slice.97
  329.5 3.8 dynamic_update_slice.97
  336.0 3.8 dynamic_update_slice.97
  342.6 3.8 dynamic_update_slice.97
  349.1 3.8 dynamic_update_slice.97
  355.7 3.8 dynamic_update_slice.97
  362.2 3.8 dynamic_update_slice.97
  368.8 3.8 dynamic_update_slice.97
  375.3 3.8 dynamic_update_slice.97
  380.6 4.7 all-to-all-start.3
  385.3 4.7 copy.180
  390.5 6.7 all-to-all-start.6
  397.2 26.2 %while.68 = (s32[]{:T(128)}, f32[4,512,512]{1,2,0:T(8,128)}, f32[4,512,4]{1,2,0:T(4,128)S(1)}, f32[4,512,4]{1,2,0:T(4,128)S(1)}, bf16[4,512,512]{2,1,0:T(8,128)(...) while((s32[]{:T(128)}, f32[4,512,512]{1,2,0:T(8,128)}, ...), condition=%wide.region_9.10_spmd.clone.clone.clone, body=%wide.region_0.9_spmd.clone.clone.sunk.clone | while | flops 550248448 | bytes 20512872 | solution.py:138
  424.4 3.9 div.25
  428.3 5.5 div.26
  436.3 7.9 all-to-all-done.6
  444.2 4.7 all-to-all-start.5
  448.9 5.7 fusion.233
  454.5 6.9 all-to-all-start.4
  461.5 4.7 reshape.159
  469.1 5.3 copy.175
  483.1 25.6 %all-to-all-done.4 = bf16[1,32,64,512]{3,1,0,2:T(8,128)(2,1)} async-done(((bf16[1,32,64,512]{3,1,0,2:T(8,128)(2,1)}), bf16[1,32,64,512]{3,1,0,2:T(8,128)(2,1)}, u32[]{:S(2)}, u32[]{:S(2)}) %all-to-all-start.4) | async-done | bytes 2097184 | tf_op jit(solution)/shard_map/all_to_all | solution.py:154
  513.3 5.2 reshape.160
  518.6 13.8 %multiply_reduce_fusion = f32[4,512,4]{2,1,0:T(8,128)} fusion(f32[4,512,4,128]{3,2,1,0:T(4,128)} %reshape.159, f32[4,512,4]{2,1,0:T(8,128)S(1)} %copy.174, f32[4,512,4,128]{3,2,1,0:T(4,128)} %reshape.160, f32[4,512,4]{2,1,0:T(8,128)} %copy.173, f32[4,512,4,128]{3,2,1,0:T(4,128)} %copy.175, f32[4,512,4]{2,1,0:T(8,128)} %copy.169), kind=kLoop, calls=%fused_computation.315 | loop fusion | flops 8380416 | bytes 12713984 | tf_op jit(solution)/shard_map/reduce_sum | solution.py:170
  534.8 5.0 all-to-all-start.7
  540.0 5.0 all-to-all-done.7
  545.9 439.5 %while.71 = (s32[]{:T(128)}, bf16[32,64,512]{2,0,1:T(8,128)(2,1)S(1)}, bf16[32,64,512]{2,0,1:T(8,128)(2,1)}, bf16[32,64,512]{2,0,1:T(8,128)(2,1)}, bf16[32,64,51...) while((s32[]{:T(128)}, ...), condition=%wide.region_24.25_spmd.clone.clone.clone, body=%wide.region_23.24_spmd.clone.clone.sunk.clone | while | flops 22020096 | bytes 2863237 | solution.py:209
  985.4 51.3 %all_to_all.171 = bf16[1,32,64,512]{3,1,0,2:T(8,128)(2,1)} all-to-all(bf16[1,32,64,512]{3,1,0,2:T(8,128)(2,1)S(1)} %bitcast.496), channel_id=1, replica_groups=mesh['seq'=16,'head'=2] {'seq'}, dimensions={2} | all-to-all | bytes 4194304 | tf_op jit(solution)/shard_map/all_to_all | solution.py:221
  1036.7 5.1 all-to-all-start.10
  1041.8 5.3 copy.154
  1047.5 41.2 %all-to-all-done.10 = bf16[1,32,64,512]{3,1,0,2:T(8,128)(2,1)S(1)} async-done(((bf16[1,32,64,512]{3,1,0,2:T(8,128)(2,1)}), bf16[1,32,64,512]{3,1,0,2:T(8,128)(2,1)S(1)}, u32[]{:S(2)}, u32[]{:S(2)}) %all-to-all-start.10) | async-done | bytes 2097184 | tf_op jit(solution)/shard_map/all_to_all | solution.py:223
  1088.6 4.7 all-to-all-start.9
  1093.3 93.9 %while.70 = (s32[]{:T(128)}, f32[4,512,512]{2,1,0:T(8,128)}, f32[4,512,512]{2,1,0:T(8,128)}, f32[4,512,512]{2,1,0:T(8,128)}, bf16[4,512,512]{2,1,0:T(8,128)(2,1)...) while((s32[]{:T(128)}, f32[4,512,512]{2,1,0:T(8,128)}, ...), condition=%wide.region_22.23_spmd.clone.clone.clone, body=%wide.region_21.22_spmd.clone.clone.sunk.clone | while | flops 1353449472 | bytes 82395496 | solution.py:203
  1187.2 4.5 div.28
  1196.9 4.1 fusion.227
  1215.3 7.1 fusion.229
  (2110 shorter events, 774.8 us)
Async XLA Ops:
  5.3 55.3 %all-to-all-start = ((bf16[16,32,4,512]{3,2,1,0:T(4,128)(2,1)}), bf16[16,32,4,512]{3,2,1,0:T(4,128)(2,1)S(1)}, u32[]{:S(2)}, u32[]{:S(2)}) async-start(bf16[16,32,4,512]{3,2,1,0:T(4,128)(2,1)} %copy.155), calls=%async_computation | async-start | bytes 4194304 | tf_op jit(solution)/shard_map/all_to_all | solution.py:123
  60.6 52.6 %all-to-all-start.1 = ((bf16[16,32,4,512]{3,2,1,0:T(4,128)(2,1)}), bf16[16,32,4,512]{3,2,1,0:T(4,128)(2,1)}, u32[]{:S(2)}, u32[]{:S(2)}) async-start(bf16[16,32,4,512]{3,2,1,0:T(4,128)(2,1)} %copy.157), calls=%async_computation.1 | async-start | bytes 4194304 | tf_op jit(solution)/shard_map/all_to_all | solution.py:126
  113.2 52.9 %all-to-all-start.2 = ((bf16[16,32,4,512]{3,2,1,0:T(4,128)(2,1)}), bf16[16,32,4,512]{3,2,1,0:T(4,128)(2,1)}, u32[]{:S(2)}, u32[]{:S(2)}) async-start(bf16[16,32,4,512]{3,2,1,0:T(4,128)(2,1)} %copy.159), calls=%async_computation.2 | async-start | bytes 4194304 | tf_op jit(solution)/shard_map/all_to_all | solution.py:129
  379.4 11.1 copy-start.21
  380.6 9.9 all-to-all-start.3
  390.5 53.7 %all-to-all-start.6 = ((bf16[16,32,4,512]{3,2,1,0:T(4,128)(2,1)}), bf16[16,32,4,512]{3,2,1,0:T(4,128)(2,1)S(1)}, u32[]{:S(2)}, u32[]{:S(2)}) async-start(bf16[16,32,4,512]{3,2,1,0:T(4,128)(2,1)} %copy.180), calls=%async_computation.6 | async-start | bytes 4194304 | tf_op jit(solution)/shard_map/all_to_all | solution.py:184
  444.2 10.4 copy-start.19
  444.2 10.4 all-to-all-start.5
  454.5 54.1 %all-to-all-start.4 = ((bf16[1,32,64,512]{3,1,0,2:T(8,128)(2,1)}), bf16[1,32,64,512]{3,1,0,2:T(8,128)(2,1)}, u32[]{:S(2)}, u32[]{:S(2)}) async-start(bf16[1,32,64,512]{3,1,0,2:T(8,128)(2,1)} %fusion.233), calls=%async_computation.4 | async-start | bytes 4194304 | tf_op jit(solution)/shard_map/all_to_all | solution.py:154
  479.5 39.1 %copy-start.12 = (f32[4,512,4]{2,1,0:T(8,128)}, f32[4,512,4]{2,1,0:T(8,128)S(1)}, u32[]{:S(2)}) copy-start(f32[4,512,4]{2,1,0:T(8,128)S(1)} %copy.174) | copy-start | bytes 98308
  534.8 10.1 all-to-all-start.7
  1036.7 51.9 %all-to-all-start.10 = ((bf16[1,32,64,512]{3,1,0,2:T(8,128)(2,1)}), bf16[1,32,64,512]{3,1,0,2:T(8,128)(2,1)S(1)}, u32[]{:S(2)}, u32[]{:S(2)}) async-start(bf16[1,32,64,512]{3,1,0,2:T(8,128)(2,1)} %bitcast.505), calls=%async_computation.10 | async-start | bytes 4194304 | tf_op jit(solution)/shard_map/all_to_all | solution.py:223
  1041.8 5.4 copy-start.15
  1088.6 4.7 copy-start.16
  1088.6 118.5 %all-to-all-start.9 = ((bf16[1,32,64,512]{3,1,0,2:T(8,128)(2,1)}), bf16[1,32,64,512]{3,1,0,2:T(8,128)(2,1)}, u32[]{:S(2)}, u32[]{:S(2)}) async-start(bf16[1,32,64,512]{3,1,0,2:T(8,128)(2,1)} %bitcast.504), calls=%async_computation.9 | async-start | bytes 4194304 | tf_op jit(solution)/shard_map/all_to_all | solution.py:222
  1095.0 3.0 copy-start
  1097.6 2.0 copy-start.2
  1107.7 6.6 copy-start.1
  1108.2 6.3 copy-start.3
  1111.8 3.0 copy-start.5
  1111.8 3.3 copy-start.7
  1118.5 3.0 copy-start
  1121.2 2.0 copy-start.2
  1131.1 6.6 copy-start.1
  1131.7 6.3 copy-start.3
  1135.2 3.0 copy-start.5
  1135.3 3.3 copy-start.7
  1141.9 3.0 copy-start
  1144.6 2.0 copy-start.2
  1154.6 6.6 copy-start.1
  1155.1 6.3 copy-start.3
  1158.7 3.0 copy-start.5
  1158.7 3.3 copy-start.7
  1165.4 3.0 copy-start
  1168.0 2.0 copy-start.2
  1178.0 6.6 copy-start.1
  1178.6 6.3 copy-start.3
  1182.1 3.0 copy-start.5
  1182.1 3.3 copy-start.7
  1187.2 4.5 copy-start.13
  1187.2 7.1 copy-start.14
  1191.7 5.2 copy-start.8
  1191.7 5.2 copy-start.11
  1196.9 4.1 copy-start.18
  1201.6 2.5 copy-start.17
  1209.3 2.2 copy-start.10
  1209.3 3.5 copy-start.20
  1212.8 2.5 copy-start.9
  (8 other events, 7.9 us)
where the time goes:
time: 1240 us; the launch traced here: 1220 us
  local copies, waits for them, and re-layouts  662 us (53%)
  waiting for transfers between devices  208 us (17%)
  matrix products  175 us (14%)
  other arithmetic  63.2 us (5%)
  starting transfers between devices  55.1 us (4%)
  blocking collectives  51.3 us (4%)
    dynamic_update_slice x320, local copies, waits for them, and re-layouts, on_device(): lax.map(lambda blocks: attend_forward(blocks[0], blocks[1], blocks[2], co...  408 us
    squeeze x128, local copies, waits for them, and re-layouts, on_device(): lax.map(lambda blocks: attend_forward(blocks[0], blocks[1], blocks[2], co...  85.5 us
    dot_general x432, matrix products, inner_last(): lax.dot_general(left, right, (((1,), (1,)), ((), ())), preferred_element_...  63.1 us
    dot_general x288, matrix products, inner_first(): lax.dot_general(left, right, (((0,), (0,)), ((), ())), preferred_element_...  53.9 us
    all_to_all x1, blocking collectives, on_device(): lax.all_to_all(shortened(col_low[0]), 'seq', split_axis=2, concat_axis=0,...  51.3 us
    dynamic_update_slice x24, local copies, waits for them, and re-layouts, on_device(): lax.map(lambda blocks: attend_forward(blocks[0], blocks[1], blocks[2], ro...  44.7 us
    all_to_all x1, waiting for transfers between devices, on_device(): lax.all_to_all(to_sending(query_rows, devices), 'seq', split_axis=0, conc...  43.5 us
    all_to_all x1, waiting for transfers between devices, on_device(): lax.all_to_all(to_sending(key_rows, devices), 'seq', split_axis=0, concat...  43 us
  transfers between devices with their start and end apart: 10, of which 8 were waited for; matrix products, arithmetic and copies ran while one was open for 16% of the time, Pallas kernels for 0%

commit v1 on v0

v1 whole, which is shorter than its diff:
```python
import functools
import math

import jax
import jax.numpy as jnp
from jax import lax
from jax.experimental import pallas as pl
from jax.experimental.pallas import tpu as pltpu
from jax.sharding import PartitionSpec as P

ROW_LEN = 512
HEAD_DIM = 128
GROUP = 8
CHUNK = 256
PIECES = 2
MASKED = -1e30
FLOOR = -1e20
LOG2E = 1.0 / math.log(2.0)
SCALE = 1.0 / math.sqrt(HEAD_DIM)
F32 = jnp.float32
BF16 = jnp.bfloat16


def dot_t(left, right):
    return lax.dot_general(left, right, (((1,), (1,)), ((), ())), preferred_element_type=F32)


def dot_f(left, right):
    return lax.dot_general(left, right, (((0,), (0,)), ((), ())), preferred_element_type=F32)


def dot(left, right):
    return jnp.dot(left, right, preferred_element_type=F32)


def row_bias(first, key_chunk, query_chunk):
    if key_chunk < query_chunk:
        return None
    keys = lax.broadcasted_iota(jnp.int32, (CHUNK, CHUNK), 0)
    queries = lax.broadcasted_iota(jnp.int32, (CHUNK, CHUNK), 1)
    return jnp.where(keys <= queries, 0.0, MASKED)


def col_bias(first, key_chunk, query_chunk):
    keys = lax.broadcasted_iota(jnp.int32, (CHUNK, CHUNK), 0)
    queries = lax.broadcasted_iota(jnp.int32, (CHUNK, CHUNK), 1)
    gap = queries - keys
    same = (gap & (GROUP - 1)) == 0
    if key_chunk == query_chunk:
        same = same & (gap > 0)
    return jnp.where(same, 0.0, MASKED)


def chunk(array, index):
    return array[index * CHUNK : (index + 1) * CHUNK]


def scores_of(query, keys, bias, query_chunk):
    out = []
    for j in range(query_chunk + 1):
        s = dot_t(chunk(keys, j), query) * (SCALE * LOG2E)
        b = bias(None, j, query_chunk)
        out.append(s if b is None else s + b)
    return out


def softmax_of(scores, values):
    top = functools.reduce(
        jnp.maximum, [jnp.max(s, axis=0, keepdims=True) for s in scores]
    )
    top = jnp.maximum(top, FLOOR)
    weights = [jnp.exp2(s - top) for s in scores]
    total = sum(jnp.sum(w, axis=0, keepdims=True) for w in weights)
    acc = sum(dot_f(chunk(values, j), w.astype(BF16)) for j, w in enumerate(weights))
    total = jnp.maximum(total, 1.0)
    return weights, top, total, acc / total


def merge(left, right):
    top = jnp.maximum(left, right)
    w_left, w_right = jnp.exp2(left - top), jnp.exp2(right - top)
    den = w_left + w_right
    return top + jnp.log2(den), w_left / den, w_right / den


def backward_of(i, probs, delta, q, k, v, g, gk, gv):
    query, grad = chunk(q, i), chunk(g, i)
    gq = None
    for j, p in enumerate(probs):
        dv = dot(p.astype(BF16), grad)
        dp = dot_t(chunk(v, j), grad)
        ds = (p * (dp - delta)).astype(BF16)
        dk = dot(ds, query)
        dq = dot_f(chunk(k, j), ds)
        gv[j] = dv if gv[j] is None else gv[j] + dv
        gk[j] = dk if gk[j] is None else gk[j] + dk
        gq = dq if gq is None else gq + dq
    return (gq * SCALE).T


def row_forward_kernel(q_ref, k_ref, v_ref, g_ref, o_ref, lse_ref, dot_ref):
    q, k, v, g = q_ref[0], k_ref[0], v_ref[0], g_ref[0]
    for i in range(q.shape[0] // CHUNK):
        span = slice(i * CHUNK, (i + 1) * CHUNK)
        _, top, total, out = softmax_of(scores_of(chunk(q, i), k, row_bias, i), v)
        o_ref[0, 0, :, span] = out
        lse_ref[0, 0, :, span] = top + jnp.log2(total)
        grad_t = chunk(g, i).astype(F32).T
        dot_ref[0, 0, :, span] = jnp.sum(grad_t * out, axis=0, keepdims=True)


def row_forward(q, k, v, g):
    rows, length, width = q.shape
    heads = width // HEAD_DIM
    block = pl.BlockSpec((1, length, HEAD_DIM), lambda r, h: (r, 0, h))
    stat = pl.BlockSpec((1, 1, 1, length), lambda r, h: (r, h, 0, 0))
    stat_shape = jax.ShapeDtypeStruct((rows, heads, 1, length), F32)
    return pl.pallas_call(
        row_forward_kernel,
        grid=(rows, heads),
        in_specs=[block] * 4,
        out_specs=[
            pl.BlockSpec((1, 1, HEAD_DIM, length), lambda r, h: (r, h, 0, 0)),
            stat,
            stat,
        ],
        out_shape=[
            jax.ShapeDtypeStruct((rows, heads, HEAD_DIM, length), F32),
            stat_shape,
            stat_shape,
        ],
        cost_estimate=pl.CostEstimate(
            flops=rows * heads * length * length * HEAD_DIM * 8,
            bytes_accessed=rows * length * width * 12,
            transcendentals=rows * heads * length * length,
        ),
        name="row_forward",
    )(q, k, v, g)


def col_kernel(x_ref, stat_ref, y_ref, lse_ref):
    devices, _, _, per, width = x_ref.shape
    tokens = devices * per
    chunks = tokens // CHUNK
    q, k, v, g = [x_ref[:, a, 0].reshape(tokens, width) for a in range(4)]
    gk, gv = [None] * chunks, [None] * chunks
    slab = CHUNK // per
    for i in range(chunks):
        span = slice(i * CHUNK, (i + 1) * CHUNK)
        here = slice(i * slab, (i + 1) * slab)
        weights, top, total, out = softmax_of(scores_of(chunk(q, i), k, col_bias, i), v)
        lse_col = top + jnp.log2(total)
        lse_ref[0, 0, :, span] = lse_col
        out_low = out.T.astype(BF16)
        y_ref[here, 0, 0] = out_low.reshape(slab, per, width)
        lse, w_row, w_col = merge(stat_ref[0, 0, 0, :, span], lse_col)
        dot_col = jnp.sum(
            (chunk(g, i).astype(F32) * out_low.astype(F32)).T, axis=0, keepdims=True
        )
        delta = w_row * stat_ref[1, 0, 0, :, span] + w_col * dot_col
        factor = jnp.exp2(top - lse)
        probs = [w * factor for w in weights]
        gq = backward_of(i, probs, delta, q, k, v, g, gk, gv)
        y_ref[here, 1, 0] = gq.astype(BF16).reshape(slab, per, width)
    for j in range(chunks):
        here = slice(j * slab, (j + 1) * slab)
        y_ref[here, 2, 0] = (gk[j] * SCALE).astype(BF16).reshape(slab, per, width)
        y_ref[here, 3, 0] = gv[j].astype(BF16).reshape(slab, per, width)


def col_both(x, stats, first_head):
    devices, kinds, groups, per, width = x.shape
    heads = width // HEAD_DIM
    tokens = devices * per
    block = pl.BlockSpec(
        (devices, kinds, 1, per, HEAD_DIM), lambda c, h: (0, 0, c, 0, h)
    )
    return pl.pallas_call(
        col_kernel,
        grid=(groups, heads),
        in_specs=[
            block,
            pl.BlockSpec((2, 1, 1, 1, tokens), lambda c, h: (0, first_head + h, c, 0, 0)),
        ],
        out_specs=[block, pl.BlockSpec((1, 1, 1, tokens), lambda c, h: (h, c, 0, 0))],
        out_shape=[
            jax.ShapeDtypeStruct(x.shape, BF16),
            jax.ShapeDtypeStruct((heads, groups, 1, tokens), F32),
        ],
        cost_estimate=pl.CostEstimate(
            flops=groups * heads * tokens * tokens * HEAD_DIM * 20,
            bytes_accessed=x.size * 4,
            transcendentals=groups * heads * tokens * tokens,
        ),
        name="col_both",
    )(x, stats)


def row_backward_kernel(
    q_ref, k_ref, v_ref, g_ref, o_ref, lse_ref, back_ref, lse_col_ref, *rest
):
    att_ref, gq_ref, gk_ref, gv_ref = rest[-4:]
    q, k, v, g = q_ref[0], k_ref[0], v_ref[0], g_ref[0]
    length = q.shape[0]
    chunks = length // CHUNK
    devices = back_ref.shape[0]
    slab = devices // chunks

    def came_back(kind, i):
        part = back_ref[i * slab : (i + 1) * slab, kind, :, 0].astype(F32)
        return part.reshape(CHUNK, HEAD_DIM)

    gk, gv = [None] * chunks, [None] * chunks
    for i in range(chunks):
        span = slice(i * CHUNK, (i + 1) * CHUNK)
        lse, w_row, w_col = merge(lse_ref[0, 0, :, span], lse_col_ref[0, 0, :, span])
        col_t = came_back(0, i).T
        att_t = o_ref[0, 0, :, span] * w_row + col_t * w_col
        low = att_t.T.astype(BF16)
        att_ref[0, span, :] = low
        delta = jnp.sum(
            (chunk(g, i).astype(F32) * low.astype(F32)).T, axis=0, keepdims=True
        )
        scores = scores_of(chunk(q, i), k, row_bias, i)
        probs = [jnp.exp2(s - lse) for s in scores]
        gq = backward_of(i, probs, delta, q, k, v, g, gk, gv)
        gq_ref[0, span, :] = (gq + came_back(1, i)).astype(BF16)
    for j in range(chunks):
        span = slice(j * CHUNK, (j + 1) * CHUNK)
        gk_ref[0, span, :] = (gk[j] * SCALE + came_back(2, j)).astype(BF16)
        gv_ref[0, span, :] = (gv[j] + came_back(3, j)).astype(BF16)


def row_backward(q, k, v, g, o, lse, back, lse_col, first_head, earlier):
    rows, length, width = q.shape
    devices, kinds, groups, _, size, piece = back.shape
    heads = piece // HEAD_DIM
    block = pl.BlockSpec((1, length, HEAD_DIM), lambda r, h: (r, 0, first_head + h))
    stat = pl.BlockSpec((1, 1, 1, length), lambda r, h: (r, first_head + h, 0, 0))
    in_specs = [block] * 4 + [
        pl.BlockSpec((1, 1, HEAD_DIM, length), lambda r, h: (r, first_head + h, 0, 0)),
        stat,
        pl.BlockSpec(
            (devices, kinds, groups, 1, size, HEAD_DIM), lambda r, h: (0, 0, 0, r, 0, h)
        ),
        pl.BlockSpec((1, 1, 1, length), lambda r, h: (r, h, 0, 0)),
    ]
    aliases = {}
    if earlier:
        aliases = {len(in_specs) + n: n for n in range(4)}
        in_specs = in_specs + [pl.BlockSpec(memory_space=pl.ANY)] * 4
    return pl.pallas_call(
        row_backward_kernel,
        grid=(rows, heads),
        in_specs=in_specs,
        out_specs=[block] * 4,
        out_shape=[jax.ShapeDtypeStruct(q.shape, BF16)] * 4,
        input_output_aliases=aliases,
        cost_estimate=pl.CostEstimate(
            flops=rows * heads * length * length * HEAD_DIM * 14,
            bytes_accessed=rows * length * piece * 28,
            transcendentals=rows * heads * length * length,
        ),
        name="row_backward",
    )(q, k, v, g, o, lse, back, lse_col, *earlier)


def exchange(array):
    return lax.all_to_all(array, "seq", split_axis=0, concat_axis=0, tiled=True)


def on_device(queries, key_vectors, value_vectors, grad_output):
    devices = lax.axis_size("seq")
    rows = queries.shape[0] // ROW_LEN
    width = queries.shape[1]
    heads = width // HEAD_DIM
    groups = ROW_LEN // devices // GROUP
    per = rows * GROUP
    tokens = devices * per
    piece = width // PIECES
    piece_heads = piece // HEAD_DIM
    arrays = (queries, key_vectors, value_vectors, grad_output)
    by_row = [a.reshape(rows, ROW_LEN, width) for a in arrays]

    arrived = []
    for n in range(PIECES):
        parts = [
            jnp.transpose(
                a[:, n * piece : (n + 1) * piece].reshape(rows, devices, groups, GROUP, piece),
                (1, 2, 0, 3, 4),
            )
            for a in arrays
        ]
        packed = jnp.stack(parts, axis=1).reshape(devices, 4, groups, per, piece)
        arrived.append(exchange(packed))

    o, lse, dots = row_forward(*by_row)
    stats = jnp.stack([lse, dots]).reshape(2, rows, heads, devices, groups, GROUP)
    stats = jnp.transpose(stats, (3, 0, 2, 4, 1, 5)).reshape(devices, -1)
    stats = exchange(stats).reshape(devices, 2, heads, groups, per)
    stats = jnp.transpose(stats, (1, 2, 3, 0, 4)).reshape(2, heads, groups, 1, tokens)

    returned = []
    for n in range(PIECES):
        y, lse_col = col_both(arrived[n], stats, n * piece_heads)
        lse_col = jnp.transpose(
            lse_col.reshape(piece_heads, groups, devices, per), (2, 0, 1, 3)
        ).reshape(devices, -1)
        lse_back = exchange(lse_col).reshape(devices, piece_heads, groups, rows, GROUP)
        lse_back = jnp.transpose(lse_back, (3, 1, 0, 2, 4)).reshape(
            rows, piece_heads, 1, ROW_LEN
        )
        back = exchange(y).reshape(devices, 4, groups, rows, GROUP, piece)
        returned.append((back, lse_back))

    outs = ()
    for n in range(PIECES):
        back, lse_back = returned[n]
        outs = row_backward(*by_row, o, lse, back, lse_back, n * piece_heads, tuple(outs))
    return tuple(a.reshape(queries.shape) for a in outs)


def solution(mesh):
    spec = P("seq", "head")
    return jax.shard_map(
        on_device,
        mesh=mesh,
        in_specs=(spec,) * 4,
        out_specs=(spec,) * 4,
        check_vma=False,
    )
```

time: 1240 us -> 482 us (0.39); the launches traced: 1220 us -> 481 us
  local copies, waits for them, and re-layouts: 662 us -> 16.4 us
  matrix products: 175 us -> 0 us
  Pallas kernels: 0 us -> 77 us
  blocking collectives: 51.3 us -> 109 us
  other arithmetic: 63.2 us -> 9.46 us
  waiting for transfers between devices: 208 us -> 237 us
  starting transfers between devices: 55.1 us -> 30.7 us
    dynamic_update_slice x344 -> x0, local copies, waits for them, and re-layouts: 453 us -> none  [the longest x320 408 us: on_device(): lax.map(lambda blocks: attend_forward(blocks[0], blocks[1], blocks[2], co...]
    dot_general x1008 -> x0, matrix products: 175 us -> none  [the longest x432 63.1 us: inner_last(): lax.dot_general(left, right, (((1,), (1,)), ((), ())), preferred_element_...]
    squeeze x180 -> x0, local copies, waits for them, and re-layouts: 107 us -> none  [the longest x128 85.5 us: on_device(): lax.map(lambda blocks: attend_forward(blocks[0], blocks[1], blocks[2], co...]
    pallas_call x0 -> x5, Pallas kernels: none -> 77 us  [the longest x2 35 us: col_both(): pl.pallas_call(col_kernel, grid=(groups, heads), in_specs=[block, pl.Bloc...]
    all_to_all x1 -> x2, blocking collectives: 51.3 us -> 109 us  [exchange(): return lax.all_to_all(array, 'seq', split_axis=0, concat_axis=0, tiled=True)]
    all_to_all x10 -> x5, waiting for transfers between devices: 208 us -> 237 us  [exchange(): return lax.all_to_all(array, 'seq', split_axis=0, concat_axis=0, tiled=True)]
    convert_element_type x8 -> x0, other arithmetic: 24.8 us -> none  [the longest x1 7.1 us: on_device(): grad_v = (row_grads[2] + from_returned(back_value).astype(jnp.float32)).a...]
    all_to_all x10 -> x5, starting transfers between devices: 55.1 us -> 30.7 us  [exchange(): return lax.all_to_all(array, 'seq', split_axis=0, concat_axis=0, tiled=True)]
  transfers between devices with their start and end apart: 10 -> 5, of which waited for: 8 -> 3; matrix products, arithmetic and copies ran while one was open for 16% -> 3% of each run, Pallas kernels for 0% -> 10%
where the time goes in v1:
time: 482 us; the launch traced here: 481 us
  waiting for transfers between devices  237 us (49%)
  blocking collectives  109 us (23%)
  Pallas kernels  77 us (16%)
  starting transfers between devices  30.7 us (6%)
  local copies, waits for them, and re-layouts  16.4 us (3%)
  other arithmetic  9.46 us (2%)
    all_to_all x5, waiting for transfers between devices, exchange(): return lax.all_to_all(array, 'seq', split_axis=0, concat_axis=0, tiled=True)  237 us
    all_to_all x2, blocking collectives, exchange(): return lax.all_to_all(array, 'seq', split_axis=0, concat_axis=0, tiled=True)  109 us
    pallas_call x2, Pallas kernels, col_both(): pl.pallas_call(col_kernel, grid=(groups, heads), in_specs=[block, pl.Bloc...  35 us
    all_to_all x5, starting transfers between devices, exchange(): return lax.all_to_all(array, 'seq', split_axis=0, concat_axis=0, tiled=True)  30.7 us
    pallas_call x2, Pallas kernels, row_backward(): pl.pallas_call(row_backward_kernel, grid=(rows, heads), in_specs=in_specs...  24.6 us
    pallas_call x1, Pallas kernels, row_forward(): pl.pallas_call(row_forward_kernel, grid=(rows, heads), in_specs=[block] *...  17.4 us
  transfers between devices with their start and end apart: 5, of which 3 were waited for; matrix products, arithmetic and copies ran while one was open for 3% of the time, Pallas kernels for 10%

profile of v1, /device:TPU:12, one launch (start us, length us, event | category | flops | bytes accessed | tf_op | source)
XLA Modules:
  0.0 480.8 jit_solution(7572135039072125192)
XLA Ops:
  0.6 17.4 %row_forward.1 = (f32[4,4,128,512]{3,2,1,0:T(8,128)}, f32[4,4,1,512]{3,2,1,0:T(1,128)}, f32[4,4,1,512]{3,2,1,0:T(1,128)}) custom-call(bf16[4,512,512]{2,1,0:T(8,128)(2,1)} %bitcast.68, bf16[4,512,512]{2,1,0:T(8,128)(2,1)} %bitcast.71, bf16[4,512,512]{2,1,0:T(8,128)(2,1)} %bitcast.74, bf16[4,512,512]{2,1,0:T(8,128)(2,1)} %bitcast.77), custom_call_target="tpu_custom_call" | custom-call | flops 4294967296 | bytes 12582912 | tf_op jit(solution)/shard_map/row_forward/pallas_call | solution.py:118
  18.0 1.0 reduce.1
  19.0 0.8 reduce
  19.9 1.4 stack.44
  21.3 1.4 stack.45
  22.8 1.5 maximum_bitcast_fusion
  24.3 1.1 copy.43
  25.4 1.8 copy.44
  27.2 7.2 %all-to-all-start.1 = ((f32[16,1,1024]{2,1,0:T(1,128)}), f32[16,1,1024]{2,1,0:T(1,128)S(1)}, u32[]{:S(2)}, u32[]{:S(2)}) async-start(f32[16,1,1024]{2,1,0:T(1,128)} %copy.44), calls=%async_computation.1 | async-start | bytes 131072 | tf_op jit(solution)/shard_map/all_to_all | solution.py:269
  34.4 0.1 fusion
  34.6 1.4 copy-done.1
  36.0 1.1 fusion.1
  37.1 0.1 fusion.2
  37.3 0.9 copy-done.3
  38.1 0.1 fusion.3
  38.3 0.3 copy_bitcast_fusion.6
  38.6 0.3 copy_bitcast_fusion.4
  38.8 2.2 pad_maximum_fusion
  41.1 6.9 %all-to-all-start = ((bf16[16,4,4,32,256]{4,3,2,1,0:T(8,128)(2,1)}), bf16[16,4,4,32,256]{4,3,2,1,0:T(8,128)(2,1)}, u32[]{:S(2)}, u32[]{:S(2)}) async-start(bf16[16,4,4,32,256]{4,3,2,1,0:T(8,128)(2,1)} %pad_maximum_fusion), calls=%async_computation | async-start | bytes 8388608 | tf_op jit(solution)/shard_map/all_to_all | solution.py:269
  48.0 1.5 copy_bitcast_fusion.2
  49.5 0.3 copy_bitcast_fusion
  49.8 2.2 pad_maximum_fusion.1
  52.0 88.9 %all-to-all-done.x_ref = bf16[16,4,4,32,256]{4,3,2,1,0:T(8,128)(2,1)} async-done(((bf16[16,4,4,32,256]{4,3,2,1,0:T(8,128)(2,1)}), bf16[16,4,4,32,256]{4,3,2,1,0:T(8,128)(2,1)}, u32[]{:S(2)}, u32[]{:S(2)}) %all-to-all-start) | async-done | bytes 4194336 | tf_op jit(solution)/shard_map/all_to_all | solution.py:269
  140.9 5.4 %all-to-all-start.4 = ((bf16[16,4,4,32,256]{4,3,2,1,0:T(8,128)(2,1)}), bf16[16,4,4,32,256]{4,3,2,1,0:T(8,128)(2,1)}, u32[]{:S(2)}, u32[]{:S(2)}) async-start(bf16[16,4,4,32,256]{4,3,2,1,0:T(8,128)(2,1)} %pad_maximum_fusion.1), calls=%async_computation.4 | async-start | bytes 8388608 | tf_op jit(solution)/shard_map/all_to_all | solution.py:269
  146.3 0.2 reduce.2
  146.5 0.2 reshape.132
  146.6 0.2 copy.45
  146.8 0.8 reshape.133.stat_ref
  147.6 17.6 %col_both.2 = (bf16[16,4,4,32,256]{4,3,2,1,0:T(8,128)(2,1)}, f32[2,4,1,512]{3,2,1,0:T(1,128)}) custom-call(bf16[16,4,4,32,256]{4,3,2,1,0:T(8,128)(2,1)} %all-to-all-done.x_ref, f32[2,4,4,1,512]{4,3,2,1,0:T(1,128)} %reshape.133.stat_ref), custom_call_target="tpu_custom_call" | custom-call | flops 5368709120 | bytes 8388608 | tf_op jit(solution)/shard_map/col_both/pallas_call | solution.py:178
  165.2 0.8 reduce.3
  166.0 0.7 all_to_all.40
  166.8 71.9 %all-to-all-done.4.x_ref = bf16[16,4,4,32,256]{4,3,2,1,0:T(8,128)(2,1)} async-done(((bf16[16,4,4,32,256]{4,3,2,1,0:T(8,128)(2,1)}), bf16[16,4,4,32,256]{4,3,2,1,0:T(8,128)(2,1)}, u32[]{:S(2)}, u32[]{:S(2)}) %all-to-all-start.4) | async-done | bytes 4194336 | tf_op jit(solution)/shard_map/all_to_all | solution.py:269
  238.7 5.5 %all-to-all-start.3 = ((f32[16,1,256]{2,1,0:T(1,128)}), f32[16,1,256]{2,1,0:T(1,128)S(1)}, u32[]{:S(2)}, u32[]{:S(2)}) async-start(f32[16,1,256]{2,1,0:T(1,128)} %all_to_all.40), calls=%async_computation.3 | async-start | bytes 32768 | tf_op jit(solution)/shard_map/all_to_all | solution.py:269
  244.2 17.4 %col_both.3 = (bf16[16,4,4,32,256]{4,3,2,1,0:T(8,128)(2,1)}, f32[2,4,1,512]{3,2,1,0:T(1,128)}) custom-call(bf16[16,4,4,32,256]{4,3,2,1,0:T(8,128)(2,1)} %all-to-all-done.4.x_ref, f32[2,4,4,1,512]{4,3,2,1,0:T(1,128)} %reshape.133.stat_ref), custom_call_target="tpu_custom_call" | custom-call | flops 5368709120 | bytes 8388608 | tf_op jit(solution)/shard_map/col_both/pallas_call | solution.py:178
  261.7 0.8 reduce.4
  262.6 0.1 all_to_all.41
  262.7 11.8 %all_to_all.49 = f32[16,1,256]{2,1,0:T(1,128)S(1)} all-to-all(f32[16,1,256]{2,1,0:T(1,128)S(1)} %all_to_all.41), channel_id=1, replica_groups=mesh['seq'=16,'head'=2] {'seq'}, dimensions={0} | all-to-all | bytes 32768 | tf_op jit(solution)/shard_map/all_to_all | solution.py:269
  274.5 97.1 %all_to_all.50 = bf16[16,4,4,32,256]{4,3,2,1,0:T(8,128)(2,1)} all-to-all(bf16[16,4,4,32,256]{4,3,2,1,0:T(8,128)(2,1)} %get-tuple-element.24), channel_id=1, replica_groups=mesh['seq'=16,'head'=2] {'seq'}, dimensions={0} | all-to-all | bytes 8388608 | tf_op jit(solution)/shard_map/all_to_all | solution.py:269
  371.7 5.6 %all-to-all-start.2 = ((bf16[16,4,4,32,256]{4,3,2,1,0:T(8,128)(2,1)}), bf16[16,4,4,32,256]{4,3,2,1,0:T(8,128)(2,1)}, u32[]{:S(2)}, u32[]{:S(2)}) async-start(bf16[16,4,4,32,256]{4,3,2,1,0:T(8,128)(2,1)} %get-tuple-element.22), calls=%async_computation.2 | async-start | bytes 8388608 | tf_op jit(solution)/shard_map/all_to_all | solution.py:269
  377.3 0.1 copy.48
  377.4 0.1 copy.49
  377.6 0.9 reshape.150.lse_col_ref
  378.4 0.1 copy.56
  378.5 0.1 copy.57
  378.7 0.9 reshape.151.lse_col_ref
  379.5 12.4 %row_backward.2 = (bf16[4,512,512]{2,1,0:T(8,128)(2,1)}, bf16[4,512,512]{2,1,0:T(8,128)(2,1)}, bf16[4,512,512]{2,1,0:T(8,128)(2,1)}, bf16[4,512,512]{2,1,0:T(8,128)(2,1)}) custom-call(bf16[4,512,512]{2,1,0:T(8,128)(2,1)} %bitcast.69, bf16[4,512,512]{2,1,0:T(8,128)(2,1)} %bitcast.72, bf16[4,512,512]{2,1,0:T(8,128)(2,1)} %bitcast.75, ...), custom_call_target="tpu_custom_call" | custom-call | flops 3758096384 | bytes 14680064 | tf_op jit(solution)/shard_map/row_backward/pallas_call | solution.py:252
  392.0 76.5 %all-to-all-done.2 = bf16[16,4,4,32,256]{4,3,2,1,0:T(8,128)(2,1)} async-done(((bf16[16,4,4,32,256]{4,3,2,1,0:T(8,128)(2,1)}), bf16[16,4,4,32,256]{4,3,2,1,0:T(8,128)(2,1)}, u32[]{:S(2)}, u32[]{:S(2)}) %all-to-all-start.2) | async-done | bytes 4194336 | tf_op jit(solution)/shard_map/all_to_all | solution.py:269
  468.4 12.2 %row_backward.3 = (bf16[4,512,512]{2,1,0:T(8,128)(2,1)}, bf16[4,512,512]{2,1,0:T(8,128)(2,1)}, bf16[4,512,512]{2,1,0:T(8,128)(2,1)}, bf16[4,512,512]{2,1,0:T(8,128)(2,1)}) custom-call(bf16[4,512,512]{2,1,0:T(8,128)(2,1)} %bitcast.70, bf16[4,512,512]{2,1,0:T(8,128)(2,1)} %bitcast.73, ...), custom_call_target="tpu_custom_call", output_to_operand_aliasing={{0}: (8, {}), {1}: (9, {}), {2}: (10, {}), {3}: (11, {})} | custom-call | flops 3758096384 | bytes 14680064 | tf_op jit(solution)/shard_map/row_backward/pallas_call | solution.py:252
  (12 shorter events, 0.2 us)
Async XLA Ops:
  18.0 16.4 %copy-start = (bf16[2048,512]{1,0:T(8,128)(2,1)S(1)}, bf16[2048,512]{1,0:T(8,128)(2,1)}, u32[]{:S(2)}) copy-start(bf16[2048,512]{1,0:T(8,128)(2,1)} %param.4) | copy-start | bytes 6291460
  27.2 13.9 %all-to-all-start.1 = ((f32[16,1,1024]{2,1,0:T(1,128)}), f32[16,1,1024]{2,1,0:T(1,128)S(1)}, u32[]{:S(2)}, u32[]{:S(2)}) async-start(f32[16,1,1024]{2,1,0:T(1,128)} %copy.44), calls=%async_computation.1 | async-start | bytes 131072 | tf_op jit(solution)/shard_map/all_to_all | solution.py:269
  34.4 1.6 copy-start.1
  34.4 2.7 copy-start.2
  36.0 2.1 copy-start.3
  41.1 99.8 %all-to-all-start = ((bf16[16,4,4,32,256]{4,3,2,1,0:T(8,128)(2,1)}), bf16[16,4,4,32,256]{4,3,2,1,0:T(8,128)(2,1)}, u32[]{:S(2)}, u32[]{:S(2)}) async-start(bf16[16,4,4,32,256]{4,3,2,1,0:T(8,128)(2,1)} %pad_maximum_fusion), calls=%async_computation | async-start | bytes 8388608 | tf_op jit(solution)/shard_map/all_to_all | solution.py:269
  140.9 97.8 %all-to-all-start.4 = ((bf16[16,4,4,32,256]{4,3,2,1,0:T(8,128)(2,1)}), bf16[16,4,4,32,256]{4,3,2,1,0:T(8,128)(2,1)}, u32[]{:S(2)}, u32[]{:S(2)}) async-start(bf16[16,4,4,32,256]{4,3,2,1,0:T(8,128)(2,1)} %pad_maximum_fusion.1), calls=%async_computation.4 | async-start | bytes 8388608 | tf_op jit(solution)/shard_map/all_to_all | solution.py:269
  238.7 24.0 %all-to-all-start.3 = ((f32[16,1,256]{2,1,0:T(1,128)}), f32[16,1,256]{2,1,0:T(1,128)S(1)}, u32[]{:S(2)}, u32[]{:S(2)}) async-start(f32[16,1,256]{2,1,0:T(1,128)} %all_to_all.40), calls=%async_computation.3 | async-start | bytes 32768 | tf_op jit(solution)/shard_map/all_to_all | solution.py:269
  371.7 96.8 %all-to-all-start.2 = ((bf16[16,4,4,32,256]{4,3,2,1,0:T(8,128)(2,1)}), bf16[16,4,4,32,256]{4,3,2,1,0:T(8,128)(2,1)}, u32[]{:S(2)}, u32[]{:S(2)}) async-start(bf16[16,4,4,32,256]{4,3,2,1,0:T(8,128)(2,1)} %get-tuple-element.22), calls=%async_computation.2 | async-start | bytes 8388608 | tf_op jit(solution)/shard_map/all_to_all | solution.py:269
